TPU v7x, 1024 devices: a whole 4x8x16 slice. The times are simulated.
1024 devices in a mesh: dp: 64 (over x, z), tensor: 16 (over y, core).
Axes of the slice: x: 4, y: 8, z: 16, core: 2. Of those that a mesh axis runs over, the one named last changes fastest.
Arguments:
- logits: bfloat16 [128, 128, 77824], P('dp', None, 'tensor'), may hold values from -110 to 290
- token_ids: int32 [128, 128], P('dp'), may hold values from 0 to 77823
- response_mask: int32 [128, 128], P('dp'), may hold values 0 or 1
- lengths: int32 [128], P('dp'), may hold values from 16 to 128
- prompt_of: int32 [128], P('dp'), may hold values from 0 to 15, as said below
- old_logprob: float32 [128, 128], P('dp'), may hold values from -14 to -10
- ref_logprob: bfloat16 [128, 128], P(None, 'dp'), may hold values from -14 to -10
- advantages: float32 [128, 128], P('dp'), may hold values from -8 to 8
- returns: float32 [128, 128], P('dp'), may hold values from -6 to 6
- critic_hidden: bfloat16 [128, 128, 5120], P(None, 'dp', 'tensor'), may hold values from -6 to 6
- value_weight: bfloat16 [5120], P('tensor'), may hold values from -0.078125 to 0.078125
Outputs:
- token_loss: float32 [128, 128], P('dp')
- critic_grad: bfloat16 [128, 128, 5120], P(None, 'dp', 'tensor')
Inputs may be any that keep to these rules, and one draw needn't show every extreme that they name: `prompt_of`: each of the 16 prompts is named by exactly 8 sequences.
All inputs are finite; a program needn't handle non-finite values. No bound on the sum of `response_mask` on one device may be relied on, other than what follows from the above.
Results may differ from a plain program's by a relative error of at most 0.001.
Values may be sent and summed in bfloat16 or wider, within the bound.
A program may use at most 32 MiB of HBM per device.

v0:
```python
import jax
import jax.numpy as jnp
from jax import lax
from jax.sharding import PartitionSpec as P

RESPONSES = 8


def sent_to_all(value, axis):
    length = lax.axis_size(axis)
    return lax.all_to_all(
        jnp.broadcast_to(value[None], (length, *value.shape)), axis, 0, 0, tiled=True
    )


def taken_together(value, axis):
    everything = sent_to_all(value, axis)
    return jnp.sum(everything, axis=0)


def together(arrays, axis):
    line, at, gathered = (jnp.concatenate([a.reshape(-1) for a in arrays]), 0, [])
    total = taken_together(line, axis)
    for a in arrays:
        gathered.append(total[at : at + a.size].reshape(a.shape))
        at += a.size
    return tuple(gathered)


def collected_together(value, axis):
    leaves = jax.tree.leaves(value)
    turns = sorted(range(len(leaves)), key=lambda k: -leaves[k].size)
    width = (1, *leaves[turns[0]].shape)[-1]
    lines = [
        jnp.pad(leaves[k].reshape(-1), (0, -leaves[k].size % width)).reshape(-1, width)
        for k in turns
    ]
    both, at, found = (sent_to_all(jnp.concatenate(lines), axis), 0, {})
    for k, line in zip(turns, lines):
        share = both[:, at : at + len(line)].reshape(len(both), -1)
        found[k] = share[:, : leaves[k].size].reshape(-1, *leaves[k].shape)
        at += len(line)
    numbers = iter(range(len(leaves)))
    return jax.tree.map(lambda _: found[next(numbers)], value)


def folded_in_pairs(pieces, combine):
    while len(jax.tree.leaves(pieces)[0]) > 1:
        pieces = jax.vmap(combine)(
            *(jax.tree.map(lambda part: part[side::2], pieces) for side in (0, 1))
        )
    return jax.tree.map(lambda part: part[0], pieces)


def joined_all(value, axis, combine):
    pieces = collected_together(value, axis)
    return folded_in_pairs(pieces, combine)


def softmax_merge(first_part, second_part):
    higher = jnp.maximum(first_part[0], second_part[0])
    summed = first_part[1] * jnp.exp(first_part[0] - higher) + second_part[1] * jnp.exp(
        second_part[0] - higher
    )
    return (higher, summed, first_part[2] + second_part[2], first_part[3] + second_part[3])


def per_device(
    logits,
    token_ids,
    response_mask,
    lengths,
    prompt_of,
    old_logprob,
    ref_logprob,
    advantages,
    returns,
    critic_hidden,
    value_weight,
):
    highest = lax.Precision.HIGHEST
    seq_rows, seq_len, vocab_width = logits.shape
    all_seqs, tile_len, feat_count = critic_hidden.shape
    dp_size = lax.axis_size("dp")
    head_weight = value_weight.astype(jnp.float32)
    tile_rows = critic_hidden.reshape(all_seqs * tile_len, feat_count)
    local_part = jnp.dot(tile_rows, value_weight, preferred_element_type=jnp.float32).reshape(
        all_seqs, tile_len
    )
    partial_value, ref_rows = (
        lax.all_to_all(local_part, "dp", split_axis=0, concat_axis=1, tiled=True),
        lax.all_to_all(
            ref_logprob.astype(jnp.float32), "dp", split_axis=0, concat_axis=1, tiled=True
        ),
    )
    position = lax.broadcasted_iota(jnp.int32, (seq_rows, seq_len), 1)
    live_mask = (response_mask * (position < lengths[:, None]).astype(jnp.int32)).astype(
        jnp.float32
    )
    prompt_count = seq_rows * dp_size // RESPONSES
    prompt_hot = (
        prompt_of[:, None] == lax.broadcasted_iota(jnp.int32, (seq_rows, prompt_count), 1)
    ).astype(jnp.float32)
    seq_tokens = jnp.sum(live_mask, axis=1)
    seq_total = jnp.sum(live_mask * advantages, axis=1)
    seq_square = jnp.sum(live_mask * advantages * advantages, axis=1)
    moments = jnp.dot(jnp.stack([seq_tokens, seq_total, seq_square]), prompt_hot, precision=highest)
    count_all, total_all, square_all = together((moments[0], moments[1], moments[2]), "dp")
    count_floor = jnp.maximum(count_all, 1.0)
    prompt_mean = total_all / count_floor
    prompt_var = (square_all - prompt_mean * total_all) / count_floor
    row_mean = jnp.dot(prompt_hot, prompt_mean, precision=highest)
    row_scale = lax.rsqrt(jnp.dot(prompt_hot, prompt_var, precision=highest) + 1.0)
    whitened = (advantages - row_mean[:, None]) * row_scale[:, None]
    local_top = jnp.max(logits, axis=2).astype(jnp.float32)
    local_sum = jnp.sum(jnp.exp(logits.astype(jnp.float32) - local_top[:, :, None]), axis=2)
    vocab_start = lax.axis_index("tensor") * vocab_width
    shifted = token_ids - vocab_start
    in_shard = (shifted >= 0) & (shifted < vocab_width)
    clipped_ids = jnp.clip(shifted, 0, vocab_width - 1)
    picked = jnp.take_along_axis(logits, clipped_ids[:, :, None], axis=2)[:, :, 0].astype(
        jnp.float32
    )
    target_part = jnp.where(in_shard, picked, 0.0)
    row_max, total_sum, target_logit, value_pred = joined_all(
        (local_top, local_sum, target_part, partial_value), "tensor", softmax_merge
    )
    logprob = target_logit - (row_max + jnp.log(total_sum))
    prob_ratio = jnp.exp(jnp.clip(logprob - old_logprob, -20.0, 20.0))
    surrogate = jnp.maximum(-whitened * prob_ratio, -whitened * jnp.clip(prob_ratio, 0.8, 1.2))
    surrogate = jnp.where(whitened < 0.0, jnp.minimum(surrogate, -3.0 * whitened), surrogate)
    ref_drift = jnp.clip(ref_rows - logprob, -20.0, 20.0)
    penalty = jnp.clip(jnp.exp(ref_drift) - ref_drift - 1.0, -10.0, 10.0)
    value_error = value_pred - returns
    token_loss = live_mask * (surrogate + 0.1 * penalty + 0.25 * value_error * value_error)
    grad_coeff = 32.0 * live_mask * value_error
    returned = lax.all_to_all(grad_coeff, "dp", split_axis=1, concat_axis=0, tiled=True)
    critic_grad = (returned[:, :, None] * head_weight[None, None, :]).astype(jnp.bfloat16)
    return (token_loss, critic_grad)


def solution(mesh):
    in_specs = (
        P("dp", None, "tensor"),
        P("dp", None),
        P("dp", None),
        P("dp"),
        P("dp"),
        P("dp", None),
        P(None, "dp"),
        P("dp", None),
        P("dp", None),
        P(None, "dp", "tensor"),
        P("tensor"),
    )
    out_specs = (P("dp", None), P(None, "dp", "tensor"))
    return jax.shard_map(
        per_device, mesh=mesh, in_specs=in_specs, out_specs=out_specs, check_vma=False
    )
```

profile of v0, /device:TPU:1, one launch (start us, length us, event | category | flops | bytes accessed | tf_op | source)
XLA Modules:
  0.0 121.9 jit_solution(2448153794413046494)
XLA Ops:
  0.6 0.0 copy-start
  0.6 1.2 %copy.31 = bf16[128,2,320]{2,1,0:T(2,128)(2,1)S(1)} copy(bf16[128,2,320]{0,2,1:T(8,128)(2,1)} %param.20) | data formatting | bytes 327680 | tf_op args[9]
  1.9 0.7 reshape.86
  2.6 0.2 fusion.2
  2.8 0.8 copy.39
  3.5 22.8 %all-to-all-start.1 = ((f32[64,2,2]{2,1,0:T(2,128)}), f32[64,2,2]{2,1,0:T(2,128)S(1)}, u32[]{:S(2)}, u32[]{:S(2)}) async-start(f32[64,2,2]{2,1,0:T(2,128)} %bitcast.16), calls=%async_computation.1 | async-start | bytes 131072 | tf_op jit(solution)/shard_map/all_to_all | solution.py:91
  26.3 0.7 fusion.39
  27.0 4.4 %gather_fusion = bf16[256]{0:T(256)(128)(2,1)S(1)} fusion(bf16[2,128,4864]{2,1,0:T(8,128)(2,1)} %param.11, s32[256]{0:T(256)S(1)} %fusion.25), kind=kCustom, calls=%fused_computation | custom fusion | bytes 4096 | tf_op jit(solution)/shard_map/jit(take_along_axis)/gather | solution.py:121
  31.4 0.0 copy-start.1
  31.4 0.0 copy-start.7
  31.5 0.0 copy-start.2
  31.5 0.0 copy-start.4
  31.5 0.0 copy-start.5
  31.5 0.0 copy-start.8
  31.5 0.0 copy-start.3
  31.5 0.0 copy-start.9
  31.5 2.1 %reduce_max.9 = bf16[2,128]{1,0:T(2,128)(2,1)S(1)} reduce(bf16[2,128,4864]{2,1,0:T(8,128)(2,1)} %param.11, bf16[]{:T(256)} %constant.23.clone.1), dimensions={2}, to_apply=%region_4.0 | reduce | flops 1244928 | bytes 2490882 | tf_op jit(solution)/shard_map/reduce_max | solution.py:115
  33.7 0.0 copy-start.6
  33.7 0.0 copy-done
  33.7 1.0 exponential_reduce_fusion
  34.7 0.0 copy-done.1
  34.7 0.0 copy-done.7
  34.7 0.1 reshape.71
  34.8 0.7 copy.33
  35.5 4.3 %all-to-all-done.1 = f32[64,2,2]{2,1,0:T(2,128)S(1)} async-done(((f32[64,2,2]{2,1,0:T(2,128)}), f32[64,2,2]{2,1,0:T(2,128)S(1)}, u32[]{:S(2)}, u32[]{:S(2)}) %all-to-all-start.1) | async-done | bytes 1056 | tf_op jit(solution)/shard_map/all_to_all | solution.py:91
  39.8 10.2 %all-to-all-start.3 = ((f32[64,2,2]{1,2,0:T(2,128)}), f32[64,2,2]{1,2,0:T(2,128)S(1)}, u32[]{:S(2)}, u32[]{:S(2)}) async-start(f32[64,2,2]{1,2,0:T(2,128)} %copy.33), calls=%async_computation.3 | async-start | bytes 131072 | tf_op jit(solution)/shard_map/all_to_all | solution.py:92
  50.0 0.1 all_to_all.50
  50.2 13.4 %all-to-all-done.3 = f32[64,2,2]{1,2,0:T(2,128)S(1)} async-done(((f32[64,2,2]{1,2,0:T(2,128)}), f32[64,2,2]{1,2,0:T(2,128)S(1)}, u32[]{:S(2)}, u32[]{:S(2)}) %all-to-all-start.3) | async-done | bytes 1056 | tf_op jit(solution)/shard_map/all_to_all | solution.py:92
  63.6 0.6 broadcast_in_dim.10
  64.2 9.5 %all-to-all-start.2 = ((f32[16,8,128]{2,1,0:T(8,128)}), f32[16,8,128]{2,1,0:T(8,128)S(1)}, u32[]{:S(2)}, u32[]{:S(2)}) async-start(f32[16,8,128]{2,1,0:T(8,128)} %broadcast_in_dim.10), calls=%async_computation.2 | async-start | bytes 131072 | tf_op jit(solution)/shard_map/all_to_all | solution.py:11
  73.8 0.0 copy-done.2
  73.8 0.1 copy.40
  73.8 7.7 %all-to-all-done.2 = f32[16,8,128]{2,1,0:T(8,128)S(1)} async-done(((f32[16,8,128]{2,1,0:T(8,128)}), f32[16,8,128]{2,1,0:T(8,128)S(1)}, u32[]{:S(2)}, u32[]{:S(2)}) %all-to-all-start.2) | async-done | bytes 65568 | tf_op jit(solution)/shard_map/all_to_all | solution.py:11
  81.6 0.0 copy-done.4
  81.7 0.0 copy-done.5
  81.7 0.0 copy-done.8
  81.7 0.1 multiply_multiply_fusion.1
  81.8 0.0 copy-done.3
  81.8 0.1 multiply_reduce_fusion.1
  81.9 0.0 copy-done.9
  81.9 0.2 fusion.4
  82.1 0.1 all_to_all.57
  82.3 0.7 copy.35
  82.9 4.6 %all-to-all-start.4 = ((f32[2,64,2]{2,0,1:T(2,128)}), f32[2,64,2]{2,0,1:T(2,128)S(1)}, u32[]{:S(2)}, u32[]{:S(2)}) async-start(f32[2,64,2]{2,0,1:T(2,128)} %copy.35), calls=%async_computation.4 | async-start | bytes 131072 | tf_op jit(solution)/shard_map/all_to_all | solution.py:137
  87.6 0.1 pad_maximum_fusion.1
  87.7 13.4 %all-to-all-done.4 = f32[2,64,2]{2,0,1:T(2,128)S(1)} async-done(((f32[2,64,2]{2,0,1:T(2,128)}), f32[2,64,2]{2,0,1:T(2,128)S(1)}, u32[]{:S(2)}, u32[]{:S(2)}) %all-to-all-start.4) | async-done | bytes 1056 | tf_op jit(solution)/shard_map/all_to_all | solution.py:137
  101.1 0.6 broadcast_in_dim.8
  101.7 5.7 %all-to-all-start = ((f32[64,1,48]{2,1,0:T(1,128)}), f32[64,1,48]{2,1,0:T(1,128)S(1)}, u32[]{:S(2)}, u32[]{:S(2)}) async-start(f32[64,1,48]{2,1,0:T(1,128)} %broadcast_in_dim.8), calls=%async_computation | async-start | bytes 65536 | tf_op jit(solution)/shard_map/all_to_all | solution.py:11
  107.4 0.1 copy.41
  107.4 0.8 multiply_convert_fusion
  108.2 12.5 %all-to-all-done = f32[64,1,48]{2,1,0:T(1,128)S(1)} async-done(((f32[64,1,48]{2,1,0:T(1,128)}), f32[64,1,48]{2,1,0:T(1,128)S(1)}, u32[]{:S(2)}, u32[]{:S(2)}) %all-to-all-start) | async-done | bytes 12320 | tf_op jit(solution)/shard_map/all_to_all | solution.py:11
  120.7 0.1 reduce_sum.48
  120.8 0.1 slice_divide_fusion
  120.9 0.2 fusion.1
  121.1 0.2 convolution_bitcast_fusion.1
  121.3 0.0 copy-done.6
  121.3 0.7 fusion.33
  (19 shorter events, 0.2 us)
Async XLA Ops:
  0.6 33.1 %copy-start = (bf16[2,128,4864]{2,1,0:T(8,128)(2,1)S(1)}, bf16[2,128,4864]{2,1,0:T(8,128)(2,1)}, u32[]{:S(2)}) copy-start(bf16[2,128,4864]{2,1,0:T(8,128)(2,1)} %param.11) | copy-start | bytes 7471108
  3.5 36.3 %all-to-all-start.1 = ((f32[64,2,2]{2,1,0:T(2,128)}), f32[64,2,2]{2,1,0:T(2,128)S(1)}, u32[]{:S(2)}, u32[]{:S(2)}) async-start(f32[64,2,2]{2,1,0:T(2,128)} %bitcast.16), calls=%async_computation.1 | async-start | bytes 131072 | tf_op jit(solution)/shard_map/all_to_all | solution.py:91
  31.4 3.2 %copy-start.1 = (s32[2,128]{1,0:T(2,128)S(1)}, s32[2,128]{1,0:T(2,128)}, u32[]{:S(2)}) copy-start(s32[2,128]{1,0:T(2,128)} %param.12) | copy-start | bytes 3076
  31.4 3.3 %copy-start.7 = (bf16[128,2]{0,1:T(2,128)(2,1)S(1)}, bf16[128,2]{0,1:T(2,128)(2,1)}, u32[]{:S(2)}) copy-start(bf16[128,2]{0,1:T(2,128)(2,1)} %param.17) | copy-start | bytes 1540
  31.5 42.3 %copy-start.2 = (bf16[320]{0:T(512)(128)(2,1)S(1)}, bf16[320]{0:T(512)(128)(2,1)}, u32[]{:S(2)}) copy-start(bf16[320]{0:T(512)(128)(2,1)} %param.21) | copy-start | bytes 1924
  31.5 50.2 %copy-start.4 = (f32[2,128]{1,0:T(2,128)S(1)}, f32[2,128]{1,0:T(2,128)}, u32[]{:S(2)}) copy-start(f32[2,128]{1,0:T(2,128)} %param.19) | copy-start | bytes 3076
  31.5 50.2 %copy-start.5 = (s32[2,128]{1,0:T(2,128)S(1)}, s32[2,128]{1,0:T(2,128)}, u32[]{:S(2)}) copy-start(s32[2,128]{1,0:T(2,128)} %param.13) | copy-start | bytes 3076
  31.5 50.2 %copy-start.8 = (s32[2]{0:T(128)S(1)}, s32[2]{0:T(128)}, u32[]{:S(2)}) copy-start(s32[2]{0:T(128)} %param.14) | copy-start | bytes 28
  31.5 50.2 %copy-start.3 = (f32[2,128]{1,0:T(2,128)S(1)}, f32[2,128]{1,0:T(2,128)}, u32[]{:S(2)}) copy-start(f32[2,128]{1,0:T(2,128)} %param.18) | copy-start | bytes 3076
  31.5 50.4 %copy-start.9 = (s32[2]{0:T(128)S(1)}, s32[2]{0:T(128)}, u32[]{:S(2)}) copy-start(s32[2]{0:T(128)} %param.15) | copy-start | bytes 28
  33.7 87.6 %copy-start.6 = (f32[2,128]{1,0:T(2,128)S(1)}, f32[2,128]{1,0:T(2,128)}, u32[]{:S(2)}) copy-start(f32[2,128]{1,0:T(2,128)} %param.16) | copy-start | bytes 3076
  39.8 23.8 %all-to-all-start.3 = ((f32[64,2,2]{1,2,0:T(2,128)}), f32[64,2,2]{1,2,0:T(2,128)S(1)}, u32[]{:S(2)}, u32[]{:S(2)}) async-start(f32[64,2,2]{1,2,0:T(2,128)} %copy.33), calls=%async_computation.3 | async-start | bytes 131072 | tf_op jit(solution)/shard_map/all_to_all | solution.py:92
  64.2 17.3 %all-to-all-start.2 = ((f32[16,8,128]{2,1,0:T(8,128)}), f32[16,8,128]{2,1,0:T(8,128)S(1)}, u32[]{:S(2)}, u32[]{:S(2)}) async-start(f32[16,8,128]{2,1,0:T(8,128)} %broadcast_in_dim.10), calls=%async_computation.2 | async-start | bytes 131072 | tf_op jit(solution)/shard_map/all_to_all | solution.py:11
  82.9 18.1 %all-to-all-start.4 = ((f32[2,64,2]{2,0,1:T(2,128)}), f32[2,64,2]{2,0,1:T(2,128)S(1)}, u32[]{:S(2)}, u32[]{:S(2)}) async-start(f32[2,64,2]{2,0,1:T(2,128)} %copy.35), calls=%async_computation.4 | async-start | bytes 131072 | tf_op jit(solution)/shard_map/all_to_all | solution.py:137
  101.7 19.0 %all-to-all-start = ((f32[64,1,48]{2,1,0:T(1,128)}), f32[64,1,48]{2,1,0:T(1,128)S(1)}, u32[]{:S(2)}, u32[]{:S(2)}) async-start(f32[64,1,48]{2,1,0:T(1,128)} %broadcast_in_dim.8), calls=%async_computation | async-start | bytes 65536 | tf_op jit(solution)/shard_map/all_to_all | solution.py:11
where the time goes:
time: 123 us; the launch traced here: 122 us
  starting transfers between devices  52.7 us (43%)
  waiting for transfers between devices  51.3 us (42%)
  local copies, waits for them, and re-layouts  10.3 us (8%)
  other arithmetic  5.84 us (5%)
    all_to_all x1, starting transfers between devices, per_device(): lax.all_to_all(local_part, 'dp', split_axis=0, concat_axis=1, tiled=True)  22.8 us
    all_to_all x2, waiting for transfers between devices, sent_to_all(): lax.all_to_all(jnp.broadcast_to(value[None], (length, *value.shape)), axi...  20.2 us
    all_to_all x2, starting transfers between devices, sent_to_all(): lax.all_to_all(jnp.broadcast_to(value[None], (length, *value.shape)), axi...  15.2 us
    all_to_all x1, waiting for transfers between devices, per_device(): lax.all_to_all(ref_logprob.astype(jnp.float32), 'dp', split_axis=0, conca...  13.4 us
    all_to_all x1, waiting for transfers between devices, per_device(): lax.all_to_all(grad_coeff, 'dp', split_axis=1, concat_axis=0, tiled=True)  13.4 us
    all_to_all x1, starting transfers between devices, per_device(): lax.all_to_all(ref_logprob.astype(jnp.float32), 'dp', split_axis=0, conca...  10.2 us
    all_to_all x1, starting transfers between devices, per_device(): lax.all_to_all(grad_coeff, 'dp', split_axis=1, concat_axis=0, tiled=True)  4.62 us
    gather x1, local copies, waits for them, and re-layouts, per_device(): jnp.take_along_axis(logits, clipped_ids[:, :, None], axis=2)[:, :, 0]  4.38 us
  transfers between devices with their start and end apart: 5, of which 5 were waited for; matrix products, arithmetic and copies ran while one was open for 8% of the time, Pallas kernels for 0%

commit v1 on v0

v1 whole, which is shorter than its diff:
```python
import functools

import jax
import jax.numpy as jnp
from jax import lax
from jax.experimental import pallas as pl
from jax.experimental.pallas import tpu as pltpu
from jax.sharding import PartitionSpec as P

MESH = pl.DeviceIdType.MESH
F32 = jnp.float32
DEAD = 1e30
BLOCK = 16


def far_first(k, half):
    back = lax.rem(k, 2)
    return half + (1 - back) * (k // 2) - back * ((k + 1) // 2)


def kernel(
    xs, zs, ys, vocab,
    logits, ids, mask, lengths, prompt_of, old, ref_t, adv, ret, critic, weight,
    loss_out, grad_out,
    lg, cr, ids_v, mask_v, old_v, ref_v, adv_v, ret_v, w_v, grad_v,
    stage, msg, inbox, quiet, idt, stt, t1_src, t1, t2_src, t2,
    lg_sem, in_sem, out_sem, dp_send, dp_recv, t1_send, t1_recv, t2_send, t2_recv,
):
    dp, tp = lax.axis_index("dp"), lax.axis_index("tensor")
    n_dp, n_tp = xs * zs, 2 * ys
    my_x, my_z, my_y, my_c = dp // zs, lax.rem(dp, zs), tp // 2, lax.rem(tp, 2)

    def dp_peer(i):
        dz, dx = far_first(i // xs, zs // 2), lax.rem(lax.rem(i, xs) + 1, xs)
        return lax.rem(my_x + dx, xs) * zs + lax.rem(my_z + dz, zs)

    def tp_peer(i):
        dy, dc = far_first(i // 2, ys // 2), lax.rem(lax.rem(i, 2) + 1, 2)
        return lax.rem(my_y + dy, ys) * 2 + lax.rem(my_c + dc, 2)

    smalls = [
        pltpu.make_async_copy(src, dst, in_sem.at[n])
        for n, (src, dst) in enumerate(
            [
                (critic, cr), (weight, w_v), (ref_t, ref_v), (mask, mask_v), (adv, adv_v),
                (ret, ret_v), (ids, ids_v), (old, old_v),
            ]
        )
    ]
    for copy in smalls:
        copy.start()
    barrier = pltpu.get_barrier_semaphore()

    def greet_dp(i, carry):
        pl.semaphore_signal(barrier, inc=1, device_id={"dp": dp_peer(i)}, device_id_type=MESH)
        return carry

    def greet_tp(i, carry):
        pl.semaphore_signal(barrier, inc=1, device_id={"tensor": tp_peer(i)}, device_id_type=MESH)
        return carry

    lax.fori_loop(0, n_dp - 1, greet_dp, 0)
    lax.fori_loop(0, n_tp - 1, greet_tp, 0)
    chunks = []
    for b in range(2):
        for h in range(2):
            rows = pl.ds(h * 64, 64)
            chunks.append(
                pltpu.make_async_copy(logits.at[b, rows], lg.at[b, rows], lg_sem.at[b * 2 + h])
            )
            chunks[-1].start()
    for copy in smalls:
        copy.wait()

    row2 = lax.broadcasted_iota(jnp.int32, (2, 128), 0)
    lane2 = lax.broadcasted_iota(jnp.int32, (2, 128), 1)
    length_of = jnp.where(row2 == 0, lengths[0], lengths[1])
    live = (mask_v[...] * (lane2 < length_of).astype(jnp.int32)).astype(F32)
    advantages, returns = adv_v[...], ret_v[...]
    live_adv = live * advantages

    def spread(column):
        return jnp.broadcast_to(jnp.sum(column, axis=1, keepdims=True), (2, 128))

    feats = w_v.shape[1]
    w_row = jnp.pad(w_v[...].astype(F32), ((0, 0), (0, -feats % 128)))
    w_all = jnp.transpose(jnp.broadcast_to(w_row, (128, w_row.shape[1])))[:feats]
    parts = [
        jnp.sum(cr[j].astype(F32) * w_all, axis=0, keepdims=True) for j in range(2)
    ]
    pid = jnp.where(row2 == 0, prompt_of[0], prompt_of[1]).astype(F32)
    lines = jnp.concatenate(
        parts
        + [
            ref_v[...].astype(F32),
            jnp.where(live > 0.0, returns, DEAD),
            spread(live),
            spread(live_adv),
            spread(live_adv * advantages),
            pid,
            jnp.zeros((114, 128), F32),
        ],
        axis=0,
    )
    stage[...] = jnp.transpose(lines)
    packed = stage[pl.ds(0, 64, stride=2), :] + pltpu.roll(stage[pl.ds(1, 64, stride=2), :], 16, 1)
    msg[...] = packed[:, None, :]
    inbox[pl.ds(dp, 1)] = msg[pl.ds(dp, 1)]

    pl.semaphore_wait(barrier, n_dp - 1 + n_tp - 1)

    def send_dp(i, carry):
        peer = dp_peer(i)
        pltpu.make_async_remote_copy(
            src_ref=msg.at[peer],
            dst_ref=inbox.at[dp],
            send_sem=dp_send,
            recv_sem=dp_recv,
            device_id={"dp": peer},
            device_id_type=MESH,
        ).start()
        return carry

    lax.fori_loop(0, n_dp - 1, send_dp, 0)

    shifted = jnp.pad((ids_v[...] - tp * vocab).astype(F32), ((0, 6), (0, 0)))
    idt[...] = jnp.transpose(shifted).astype(jnp.int32)
    stt[...] = jnp.zeros((128, 128), F32)
    lane = lax.broadcasted_iota(jnp.int32, (BLOCK, 128), 1)
    for b in range(2):
        for h in range(2):
            chunks[b * 2 + h].wait()

            def token_block(i, carry):
                rows = pl.ds(pl.multiple_of(h * 64 + i * BLOCK, BLOCK), BLOCK)
                top = lg[b, rows, pl.ds(0, 128)]
                for c in range(1, vocab // 128):
                    top = jnp.maximum(top, lg[b, rows, pl.ds(c * 128, 128)])
                top = jnp.max(top.astype(F32), axis=1, keepdims=True)
                tops = jnp.broadcast_to(top, (BLOCK, 128))
                wanted = jnp.broadcast_to(idt[rows, b : b + 1], (BLOCK, 128))
                total = jnp.zeros((BLOCK, 128), F32)
                found = jnp.zeros((BLOCK, 128), F32)
                for c in range(vocab // 128):
                    x = lg[b, rows, pl.ds(c * 128, 128)].astype(F32)
                    total = total + jnp.exp(x - tops)
                    found = jnp.where(wanted == lane + c * 128, x, found)
                stt[rows, b : b + 1] = top
                stt[rows, 2 + b : 3 + b] = jnp.sum(total, axis=1, keepdims=True)
                stt[rows, 4 + b : 5 + b] = jnp.sum(found, axis=1, keepdims=True)
                return carry

            lax.fori_loop(0, 64 // BLOCK, token_block, 0)
    t1_src[0:6] = jnp.transpose(stt[...])[0:6]
    t1_src[6:8] = jnp.concatenate(parts, axis=0)
    t1[pl.ds(tp, 1)] = t1_src[...][None]

    def send_t1(i, carry):
        pltpu.make_async_remote_copy(
            src_ref=t1_src,
            dst_ref=t1.at[tp],
            send_sem=t1_send,
            recv_sem=t1_recv,
            device_id={"tensor": tp_peer(i)},
            device_id_type=MESH,
        ).start()
        return carry

    lax.fori_loop(0, n_tp - 1, send_t1, 0)

    def all_but_one(ref, sem):
        some = ref.at[pl.ds(0, ref.shape[0] - 1)]
        return pltpu.make_async_copy(some, some, sem)

    all_but_one(inbox, dp_recv).wait()
    got = inbox[...][:, 0, :]
    quiet[pl.ds(0, 64, stride=2), :] = got
    quiet[pl.ds(1, 64, stride=2), :] = pltpu.roll(got, 127, 1)
    turned = jnp.transpose(quiet[...])

    def pair(k):
        return jnp.concatenate([turned[k : k + 1], turned[16 + k : 17 + k]], axis=0)

    t2_src[...] = pair(0)
    t2[pl.ds(tp, 1)] = t2_src[...][None]

    def send_t2(i, carry):
        pltpu.make_async_remote_copy(
            src_ref=t2_src,
            dst_ref=t2.at[tp],
            send_sem=t2_send,
            recv_sem=t2_recv,
            device_id={"tensor": tp_peer(i)},
            device_id_type=MESH,
        ).start()
        return carry

    lax.fori_loop(0, n_tp - 1, send_t2, 0)

    ref_rows, held_returns = pair(2), pair(4)
    same = (turned[12:13] == pid).astype(F32)
    count = jnp.sum(same * turned[6:7], axis=1, keepdims=True)
    summed = jnp.sum(same * turned[8:9], axis=1, keepdims=True)
    square = jnp.sum(same * turned[10:11], axis=1, keepdims=True)
    floor = jnp.maximum(count, 1.0)
    mean = summed / floor
    var = (square - mean * summed) / floor
    whitened = (advantages - mean) * lax.rsqrt(var + 1.0)

    all_but_one(t1, t1_recv).wait()
    shards = t1[...]
    values = jnp.sum(shards[:, 6:8], axis=0)
    coeff = jnp.where(held_returns > 1e29, 0.0, 32.0 * (values - held_returns))
    for j in range(2):
        grad_v[j] = (w_all * coeff[j : j + 1]).astype(jnp.bfloat16)
    grad_copy = pltpu.make_async_copy(grad_v, grad_out, out_sem)
    grad_copy.start()

    tops = shards[:, 0:2]
    row_max = jnp.max(tops, axis=0)
    total = jnp.sum(shards[:, 2:4] * jnp.exp(tops - row_max[None]), axis=0)
    target = jnp.sum(shards[:, 4:6], axis=0)
    logprob = target - (row_max + jnp.log(total))
    ratio = jnp.exp(jnp.clip(logprob - old_v[...], -20.0, 20.0))
    surrogate = jnp.maximum(-whitened * ratio, -whitened * jnp.clip(ratio, 0.8, 1.2))
    surrogate = jnp.where(whitened < 0.0, jnp.minimum(surrogate, -3.0 * whitened), surrogate)
    drift = jnp.clip(ref_rows - logprob, -20.0, 20.0)
    penalty = jnp.clip(jnp.exp(drift) - drift - 1.0, -10.0, 10.0)
    policy = surrogate + 0.1 * penalty

    all_but_one(t2, t2_recv).wait()
    error = jnp.sum(t2[...], axis=0) - returns
    loss_out[...] = live * (policy + 0.25 * error * error)

    all_but_one(inbox, dp_send).wait()
    all_but_one(t1, t1_send).wait()
    all_but_one(t2, t2_send).wait()
    grad_copy.wait()


def per_device(sizes, *arrays):
    (
        logits, ids, mask, lengths, prompt_of, old, ref, adv, ret, critic, weight
    ) = arrays
    seqs, length, vocab = logits.shape
    batch, tile, feats = critic.shape
    xs, zs, ys = sizes
    any_ref, smem = pl.BlockSpec(memory_space=pl.ANY), pl.BlockSpec(memory_space=pltpu.SMEM)
    dma = pltpu.SemaphoreType.DMA
    vm = pltpu.VMEM
    loss, grad = pl.pallas_call(
        functools.partial(kernel, xs, zs, ys, vocab),
        out_shape=(
            jax.ShapeDtypeStruct((seqs, length), F32),
            jax.ShapeDtypeStruct((tile, feats, batch), jnp.bfloat16),
        ),
        in_specs=[any_ref] * 3 + [smem] * 2 + [any_ref] * 6,
        out_specs=(pl.BlockSpec(memory_space=pltpu.VMEM), any_ref),
        scratch_shapes=[
            vm(logits.shape, jnp.bfloat16),
            vm((tile, feats, batch), jnp.bfloat16),
            vm((seqs, length), jnp.int32),
            vm((seqs, length), jnp.int32),
            vm((seqs, length), F32),
            vm((tile, batch), jnp.bfloat16),
            vm((seqs, length), F32),
            vm((seqs, length), F32),
            vm((1, feats), jnp.bfloat16),
            vm((tile, feats, batch), jnp.bfloat16),
            vm((128, 128), F32),
            vm((64, 1, 128), F32),
            vm((64, 1, 128), F32),
            vm((128, 128), F32),
            vm((128, 8), jnp.int32),
            vm((128, 128), F32),
            vm((8, 128), F32),
            vm((2 * ys, 8, 128), F32),
            vm((seqs, length), F32),
            vm((2 * ys, seqs, length), F32),
            dma((4,)), dma((8,)), dma, dma, dma, dma, dma, dma, dma,
        ],
        compiler_params=pltpu.CompilerParams(collective_id=0, has_side_effects=True),
        name="ppo_all",
    )(
        logits, ids, mask, lengths, prompt_of, old, ref.T, adv, ret,
        jnp.transpose(critic, (1, 2, 0)), weight.reshape(1, feats),
    )
    return loss, jnp.transpose(grad, (2, 0, 1))


def solution(mesh):
    in_specs = (
        P("dp", None, "tensor"),
        P("dp", None),
        P("dp", None),
        P("dp"),
        P("dp"),
        P("dp", None),
        P(None, "dp"),
        P("dp", None),
        P("dp", None),
        P(None, "dp", "tensor"),
        P("tensor"),
    )
    out_specs = (P("dp", None), P(None, "dp", "tensor"))
    dp_size, tp_size = mesh.shape["dp"], mesh.shape["tensor"]
    sizes = (4, dp_size // 4, tp_size // 2)
    return jax.shard_map(
        functools.partial(per_device, sizes),
        mesh=mesh,
        in_specs=in_specs,
        out_specs=out_specs,
        check_vma=False,
    )
```

time: 123 us -> 44.8 us (0.36)
  starting transfers between devices: 52.7 us -> 0 us
  waiting for transfers between devices: 51.3 us -> 0 us
  Pallas kernels: 0 us -> 39.9 us
  local copies, waits for them, and re-layouts: 10.3 us -> 4.04 us
  other arithmetic: 5.84 us -> 0 us
    all_to_all x5 -> x0, starting transfers between devices: 52.7 us -> none  [the longest x1 22.8 us: per_device(): lax.all_to_all(local_part, 'dp', split_axis=0, concat_axis=1, tiled=True)]
    all_to_all x5 -> x0, waiting for transfers between devices: 51.3 us -> none  [the longest x2 20.2 us: sent_to_all(): lax.all_to_all(jnp.broadcast_to(value[None], (length, *value.shape)), axi...]
    pallas_call x0 -> x1, Pallas kernels: none -> 39.9 us  [per_device(): pl.pallas_call(functools.partial(kernel, xs, zs, ys, vocab), out_shape=(j...]
    gather x1 -> x0, local copies, waits for them, and re-layouts: 4.38 us -> none  [per_device(): jnp.take_along_axis(logits, clipped_ids[:, :, None], axis=2)[:, :, 0]]
    reduce_max x1 -> x0, other arithmetic: 2.15 us -> none  [per_device(): local_top = jnp.max(logits, axis=2).astype(jnp.float32)]
    all_to_all x7 -> x0, local copies, waits for them, and re-layouts: 1.83 us -> none  [the longest x3 0.86 us: per_device(): lax.all_to_all(ref_logprob.astype(jnp.float32), 'dp', split_axis=0, conca...]
    broadcast_in_dim x2 -> x0, local copies, waits for them, and re-layouts: 1.26 us -> none  [sent_to_all(): jnp.broadcast_to(value[None], (length, *value.shape))]
    reshape x0 -> x1, local copies, waits for them, and re-layouts: none -> 1.24 us  [per_device(): weight.reshape(1, feats)]
  transfers between devices with their start and end apart: 5 -> 0, of which waited for: 5 -> 0; matrix products, arithmetic and copies ran while one was open for 8% -> 0% of each run, Pallas kernels for 0% -> 0%
where the time goes in v1:
time: 44.8 us; the launch traced here: 44.6 us
  Pallas kernels  39.9 us (89%)
  local copies, waits for them, and re-layouts  4.04 us (9%)
  between operations  0.64 us (1%)
    pallas_call x1, Pallas kernels, per_device(): pl.pallas_call(functools.partial(kernel, xs, zs, ys, vocab), out_shape=(j...  39.9 us
    unnamed x2, local copies, waits for them, and re-layouts  2.79 us
    reshape x1, local copies, waits for them, and re-layouts, per_device(): weight.reshape(1, feats)  1.24 us

profile of v1, /device:TPU:1, one launch (start us, length us, event | category | flops | bytes accessed | tf_op | source)
XLA Modules:
  0.0 44.6 jit_solution(15554507319729278531)
XLA Ops:
  0.6 1.2 %reshape.7.weight = bf16[1,320]{1,0:T(2,128)(2,1)} reshape(bf16[320]{0:T(512)(128)(2,1)} %param.21) | data formatting | bytes 1280 | tf_op jit(solution)/shard_map/reshape | solution.py:286
  1.9 39.9 %ppo_all.1 = (f32[2,128]{1,0:T(2,128)}, bf16[2,320,128]{2,1,0:T(8,128)(2,1)}) custom-call(bf16[2,128,4864]{2,1,0:T(8,128)(2,1)} %logits.1, s32[2,128]{1,0:T(2,128)} %ids.1, s32[2,128]{1,0:T(2,128)} %mask.1, s32[2]{0:T(128)} %lengths.1, s32[2]{0:T(128)} %prompt_of.1, f32[2,128]{1,0:T(2,128)} %old.1, bf16[2,128]{1,0:T(2,128)(2,1)} %bitcast.5, f32[2,128]{1,0:T(2,128)} %adv.1, ...), custom_call_target="tpu_custom_call" | custom-call | tf_op jit(solution)/shard_map/ppo_all/pallas_call | solution.py:251
  41.8 1.2 %copy.15 = f32[2,128]{1,0:T(2,128)} copy(f32[2,128]{1,0:T(2,128)} %get-tuple-element.8) | data formatting | bytes 2048
  43.0 1.6 %copy.16 = bf16[128,2,320]{0,2,1:T(8,128)(2,1)} copy(bf16[128,2,320]{0,2,1:T(8,128)(2,1)} %bitcast.3) | data formatting | bytes 327680

commit v2 on v1

--- a/solution.py
+++ b/solution.py
@@ -1,4 +1,5 @@
 import functools
+import itertools
 
 import jax
 import jax.numpy as jnp
@@ -13,54 +14,47 @@
 BLOCK = 16
 
 
-def far_first(k, half):
-    back = lax.rem(k, 2)
-    return half + (1 - back) * (k // 2) - back * ((k + 1) // 2)
+def far_first(*sizes):
+    offsets = itertools.product(*(range(n) for n in sizes))
+    return sorted(offsets, key=lambda o: -sum(min(d, n - d) for d, n in zip(o, sizes)))[:-1]
 
 
 def kernel(
     xs, zs, ys, vocab,
-    logits, ids, mask, lengths, prompt_of, old, ref_t, adv, ret, critic, weight,
+    logits, ids, mask, lengths_in, prompt_in, old, ref_t, adv, ret, critic, weight,
     loss_out, grad_out,
-    lg, cr, ids_v, mask_v, old_v, ref_v, adv_v, ret_v, w_v, grad_v,
+    lg, cr, ids_v, mask_v, old_v, ref_v, adv_v, ret_v, w_v, lengths, prompt_of,
     stage, msg, inbox, quiet, idt, stt, t1_src, t1, t2_src, t2,
-    lg_sem, in_sem, out_sem, dp_send, dp_recv, t1_send, t1_recv, t2_send, t2_recv,
+    lg_sem, in_sem, dp_send, dp_recv, t1_send, t1_recv, t2_send, t2_recv,
 ):
     dp, tp = lax.axis_index("dp"), lax.axis_index("tensor")
     n_dp, n_tp = xs * zs, 2 * ys
     my_x, my_z, my_y, my_c = dp // zs, lax.rem(dp, zs), tp // 2, lax.rem(tp, 2)
-
-    def dp_peer(i):
-        dz, dx = far_first(i // xs, zs // 2), lax.rem(lax.rem(i, xs) + 1, xs)
-        return lax.rem(my_x + dx, xs) * zs + lax.rem(my_z + dz, zs)
-
-    def tp_peer(i):
-        dy, dc = far_first(i // 2, ys // 2), lax.rem(lax.rem(i, 2) + 1, 2)
-        return lax.rem(my_y + dy, ys) * 2 + lax.rem(my_c + dc, 2)
 
     smalls = [
         pltpu.make_async_copy(src, dst, in_sem.at[n])
         for n, (src, dst) in enumerate(
             [
                 (critic, cr), (weight, w_v), (ref_t, ref_v), (mask, mask_v), (adv, adv_v),
-                (ret, ret_v), (ids, ids_v), (old, old_v),
+                (lengths_in, lengths), (prompt_in, prompt_of), (ret, ret_v), (ids, ids_v), (old, old_v),
             ]
         )
     ]
     for copy in smalls:
         copy.start()
+    at_x = [lax.rem(my_x + d, xs) * zs for d in range(xs)]
+    at_z = [lax.rem(my_z + d, zs) for d in range(zs)]
+    at_y = [lax.rem(my_y + d, ys) * 2 for d in range(ys)]
+    at_c = [my_c, 1 - my_c]
+    dp_peers = [at_x[x] + at_z[z] for x, z in far_first(xs, zs)]
+    tp_peers = [at_y[y] + at_c[c] for y, c in far_first(ys, 2)]
+
     barrier = pltpu.get_barrier_semaphore()
 
-    def greet_dp(i, carry):
-        pl.semaphore_signal(barrier, inc=1, device_id={"dp": dp_peer(i)}, device_id_type=MESH)
-        return carry
-
-    def greet_tp(i, carry):
-        pl.semaphore_signal(barrier, inc=1, device_id={"tensor": tp_peer(i)}, device_id_type=MESH)
-        return carry
-
-    lax.fori_loop(0, n_dp - 1, greet_dp, 0)
-    lax.fori_loop(0, n_tp - 1, greet_tp, 0)
+    for peer in dp_peers:
+        pl.semaphore_signal(barrier, inc=1, device_id={"dp": peer}, device_id_type=MESH)
+    for peer in tp_peers:
+        pl.semaphore_signal(barrier, inc=1, device_id={"tensor": peer}, device_id_type=MESH)
     chunks = []
     for b in range(2):
         for h in range(2):
@@ -82,8 +76,8 @@
     def spread(column):
         return jnp.broadcast_to(jnp.sum(column, axis=1, keepdims=True), (2, 128))
 
-    feats = w_v.shape[1]
-    w_row = jnp.pad(w_v[...].astype(F32), ((0, 0), (0, -feats % 128)))
+    feats = w_v.shape[0]
+    w_row = jnp.pad(w_v[...].astype(F32).reshape(1, feats), ((0, 0), (0, -feats % 128)))
     w_all = jnp.transpose(jnp.broadcast_to(w_row, (128, w_row.shape[1])))[:feats]
     parts = [
         jnp.sum(cr[j].astype(F32) * w_all, axis=0, keepdims=True) for j in range(2)
@@ -109,8 +103,7 @@
 
     pl.semaphore_wait(barrier, n_dp - 1 + n_tp - 1)
 
-    def send_dp(i, carry):
-        peer = dp_peer(i)
+    for peer in dp_peers:
         pltpu.make_async_remote_copy(
             src_ref=msg.at[peer],
             dst_ref=inbox.at[dp],
@@ -119,9 +112,6 @@
             device_id={"dp": peer},
             device_id_type=MESH,
         ).start()
-        return carry
-
-    lax.fori_loop(0, n_dp - 1, send_dp, 0)
 
     shifted = jnp.pad((ids_v[...] - tp * vocab).astype(F32), ((0, 6), (0, 0)))
     idt[...] = jnp.transpose(shifted).astype(jnp.int32)
@@ -155,18 +145,15 @@
     t1_src[6:8] = jnp.concatenate(parts, axis=0)
     t1[pl.ds(tp, 1)] = t1_src[...][None]
 
-    def send_t1(i, carry):
+    for peer in tp_peers:
         pltpu.make_async_remote_copy(
             src_ref=t1_src,
             dst_ref=t1.at[tp],
             send_sem=t1_send,
             recv_sem=t1_recv,
-            device_id={"tensor": tp_peer(i)},
+            device_id={"tensor": peer},
             device_id_type=MESH,
         ).start()
-        return carry
-
-    lax.fori_loop(0, n_tp - 1, send_t1, 0)
 
     def all_but_one(ref, sem):
         some = ref.at[pl.ds(0, ref.shape[0] - 1)]
@@ -184,18 +171,15 @@
     t2_src[...] = pair(0)
     t2[pl.ds(tp, 1)] = t2_src[...][None]
 
-    def send_t2(i, carry):
+    for peer in tp_peers:
         pltpu.make_async_remote_copy(
             src_ref=t2_src,
             dst_ref=t2.at[tp],
             send_sem=t2_send,
             recv_sem=t2_recv,
-            device_id={"tensor": tp_peer(i)},
+            device_id={"tensor": peer},
             device_id_type=MESH,
         ).start()
-        return carry
-
-    lax.fori_loop(0, n_tp - 1, send_t2, 0)
 
     ref_rows, held_returns = pair(2), pair(4)
     same = (turned[12:13] == pid).astype(F32)
@@ -212,9 +196,7 @@
     values = jnp.sum(shards[:, 6:8], axis=0)
     coeff = jnp.where(held_returns > 1e29, 0.0, 32.0 * (values - held_returns))
     for j in range(2):
-        grad_v[j] = (w_all * coeff[j : j + 1]).astype(jnp.bfloat16)
-    grad_copy = pltpu.make_async_copy(grad_v, grad_out, out_sem)
-    grad_copy.start()
+        grad_out[j] = (w_all * coeff[j : j + 1]).astype(jnp.bfloat16)
 
     tops = shards[:, 0:2]
     row_max = jnp.max(tops, axis=0)
@@ -226,16 +208,27 @@
     surrogate = jnp.where(whitened < 0.0, jnp.minimum(surrogate, -3.0 * whitened), surrogate)
     drift = jnp.clip(ref_rows - logprob, -20.0, 20.0)
     penalty = jnp.clip(jnp.exp(drift) - drift - 1.0, -10.0, 10.0)
-    policy = surrogate + 0.1 * penalty
+    policy = live * (surrogate + 0.1 * penalty)
+    scale = 0.25 * live
 
     all_but_one(t2, t2_recv).wait()
     error = jnp.sum(t2[...], axis=0) - returns
-    loss_out[...] = live * (policy + 0.25 * error * error)
+    loss_out[...] = policy + scale * error * error
 
     all_but_one(inbox, dp_send).wait()
     all_but_one(t1, t1_send).wait()
     all_but_one(t2, t2_send).wait()
-    grad_copy.wait()
+
+
+def finish(loss, grad, loss_out, grad_out, sems):
+    copies = [
+        pltpu.make_async_copy(src, dst, sems.at[n])
+        for n, (src, dst) in enumerate([(grad, grad_out), (loss, loss_out)])
+    ]
+    for copy in copies:
+        copy.start()
+    for copy in copies:
+        copy.wait()
 
 
 def per_device(sizes, *arrays):
@@ -245,17 +238,17 @@
     seqs, length, vocab = logits.shape
     batch, tile, feats = critic.shape
     xs, zs, ys = sizes
-    any_ref, smem = pl.BlockSpec(memory_space=pl.ANY), pl.BlockSpec(memory_space=pltpu.SMEM)
+    any_ref, vmem = pl.BlockSpec(memory_space=pl.ANY), pl.BlockSpec(memory_space=pltpu.VMEM)
     dma = pltpu.SemaphoreType.DMA
     vm = pltpu.VMEM
     loss, grad = pl.pallas_call(
         functools.partial(kernel, xs, zs, ys, vocab),
         out_shape=(
-            jax.ShapeDtypeStruct((seqs, length), F32),
-            jax.ShapeDtypeStruct((tile, feats, batch), jnp.bfloat16),
+            vm((seqs, length), F32),
+            vm((tile, feats, batch), jnp.bfloat16),
         ),
-        in_specs=[any_ref] * 3 + [smem] * 2 + [any_ref] * 6,
-        out_specs=(pl.BlockSpec(memory_space=pltpu.VMEM), any_ref),
+        in_specs=[any_ref] * 11,
+        out_specs=[vmem] * 2,
         scratch_shapes=[
             vm(logits.shape, jnp.bfloat16),
             vm((tile, feats, batch), jnp.bfloat16),
@@ -265,8 +258,9 @@
             vm((tile, batch), jnp.bfloat16),
             vm((seqs, length), F32),
             vm((seqs, length), F32),
-            vm((1, feats), jnp.bfloat16),
-            vm((tile, feats, batch), jnp.bfloat16),
+            vm((feats,), jnp.bfloat16),
+            pltpu.SMEM((seqs,), jnp.int32),
+            pltpu.SMEM((seqs,), jnp.int32),
             vm((128, 128), F32),
             vm((64, 1, 128), F32),
             vm((64, 1, 128), F32),
@@ -277,14 +271,26 @@
             vm((2 * ys, 8, 128), F32),
             vm((seqs, length), F32),
             vm((2 * ys, seqs, length), F32),
-            dma((4,)), dma((8,)), dma, dma, dma, dma, dma, dma, dma,
+            dma((4,)), dma((10,)), dma, dma, dma, dma, dma, dma,
         ],
         compiler_params=pltpu.CompilerParams(collective_id=0, has_side_effects=True),
         name="ppo_all",
     )(
         logits, ids, mask, lengths, prompt_of, old, ref.T, adv, ret,
-        jnp.transpose(critic, (1, 2, 0)), weight.reshape(1, feats),
+        jnp.transpose(critic, (1, 2, 0)), weight,
     )
+    loss, grad = pl.pallas_call(
+        finish,
+        out_shape=(
+            jax.ShapeDtypeStruct((seqs, length), F32),
+            jax.ShapeDtypeStruct((tile, feats, batch), jnp.bfloat16),
+        ),
+        in_specs=[vmem] * 2,
+        out_specs=[any_ref] * 2,
+        scratch_shapes=[dma((2,))],
+        compiler_params=pltpu.CompilerParams(vmem_limit_bytes=2**20),
+        name="ppo_finish",
+    )(loss, grad)
     return loss, jnp.transpose(grad, (2, 0, 1))
 
 

time: 44.8 us -> 40 us (0.89)
  local copies, waits for them, and re-layouts: 4.04 us -> 0 us
  Pallas kernels: 39.9 us -> 39.2 us
    unnamed x2 -> x0, local copies, waits for them, and re-layouts: 2.79 us -> none
    reshape x1 -> x0, local copies, waits for them, and re-layouts: 1.24 us -> none  [per_device(): weight.reshape(1, feats)]
    pallas_call x1 -> x2, Pallas kernels: 39.9 us -> 39.2 us  [the longest x1 38.5 us: per_device(): pl.pallas_call(functools.partial(kernel, xs, zs, ys, vocab), out_shape=(v...]
where the time goes in v2:
time: 40 us; the launch traced here: 39.9 us
  Pallas kernels  39.2 us (98%)
  between operations  0.64 us (2%)
    pallas_call x1, Pallas kernels, per_device(): pl.pallas_call(functools.partial(kernel, xs, zs, ys, vocab), out_shape=(v...  38.5 us

profile of v2, /device:TPU:1, one launch (start us, length us, event | category | flops | bytes accessed | tf_op | source)
XLA Modules:
  0.0 39.9 jit_solution(900732745726657759)
XLA Ops:
  0.6 38.5 %ppo_all.1 = (f32[2,128]{1,0:T(2,128)S(1)}, bf16[2,320,128]{2,1,0:T(8,128)(2,1)S(1)}) custom-call(bf16[2,128,4864]{2,1,0:T(8,128)(2,1)} %logits.1, s32[2,128]{1,0:T(2,128)} %ids.1, s32[2,128]{1,0:T(2,128)} %mask.1, s32[2]{0:T(128)} %lengths_in.1, s32[2]{0:T(128)} %prompt_in.1, f32[2,128]{1,0:T(2,128)} %old.1, bf16[2,128]{1,0:T(2,128)(2,1)} %bitcast.4, ...), custom_call_target="tpu_custom_call" | custom-call | tf_op jit(solution)/shard_map/ppo_all/pallas_call | solution.py:244
  39.2 0.7 %ppo_finish.1 = (f32[2,128]{1,0:T(2,128)}, bf16[2,320,128]{2,1,0:T(8,128)(2,1)}) custom-call(f32[2,128]{1,0:T(2,128)S(1)} %get-tuple-element.6.loss, bf16[2,320,128]{2,1,0:T(8,128)(2,1)S(1)} %get-tuple-element.7.grad), custom_call_target="tpu_custom_call" | custom-call | tf_op jit(solution)/shard_map/ppo_finish/pallas_call | solution.py:282

commit v3 on v2

--- a/solution.py
+++ b/solution.py
@@ -24,8 +24,9 @@
     logits, ids, mask, lengths_in, prompt_in, old, ref_t, adv, ret, critic, weight,
     loss_out, grad_out,
     lg, cr, ids_v, mask_v, old_v, ref_v, adv_v, ret_v, w_v, lengths, prompt_of,
-    stage, msg, inbox, quiet, idt, stt, t1_src, t1, t2_src, t2,
+    stage, msg, inbox, relay, quiet, idt, stt, t1_src, t1, t2_src, t2,
     lg_sem, in_sem, dp_send, dp_recv, t1_send, t1_recv, t2_send, t2_recv,
+    relay_send, relay_recv, entered, line_in,
 ):
     dp, tp = lax.axis_index("dp"), lax.axis_index("tensor")
     n_dp, n_tp = xs * zs, 2 * ys
@@ -47,14 +48,26 @@
     at_y = [lax.rem(my_y + d, ys) * 2 for d in range(ys)]
     at_c = [my_c, 1 - my_c]
     dp_peers = [at_x[x] + at_z[z] for x, z in far_first(xs, zs)]
+    half = zs // 2
+    near, far = my_z < half, my_z >= half
+    partner = my_x * zs + (zs - 1 - my_z)
+    at_near = [lax.rem(my_z + d, half) for d in range(half)]
+    near_peers = [
+        (at_x[x] + at_near[z], at_x[x] + (zs - 1 - at_near[z])) for x, z in far_first(xs, half)
+    ]
+    own_column = (my_x * zs + at_near[0], my_x * zs + (zs - 1 - at_near[0]))
+
     tp_peers = [at_y[y] + at_c[c] for y, c in far_first(ys, 2)]
 
     barrier = pltpu.get_barrier_semaphore()
 
-    for peer in dp_peers:
-        pl.semaphore_signal(barrier, inc=1, device_id={"dp": peer}, device_id_type=MESH)
-    for peer in tp_peers:
-        pl.semaphore_signal(barrier, inc=1, device_id={"tensor": peer}, device_id_type=MESH)
+    @pl.when(near)
+    def _():
+        for peer in dp_peers:
+            pl.semaphore_signal(barrier, inc=1, device_id={"dp": peer}, device_id_type=MESH)
+        for peer in tp_peers:
+            pl.semaphore_signal(barrier, inc=1, device_id={"tensor": peer}, device_id_type=MESH)
+
     chunks = []
     for b in range(2):
         for h in range(2):
@@ -99,19 +112,36 @@
     stage[...] = jnp.transpose(lines)
     packed = stage[pl.ds(0, 64, stride=2), :] + pltpu.roll(stage[pl.ds(1, 64, stride=2), :], 16, 1)
     msg[...] = packed[:, None, :]
-    inbox[pl.ds(dp, 1)] = msg[pl.ds(dp, 1)]
-
-    pl.semaphore_wait(barrier, n_dp - 1 + n_tp - 1)
-
-    for peer in dp_peers:
+
+    @pl.when(near)
+    def _():
+        inbox[pl.ds(dp, 1)] = msg[pl.ds(dp, 1)]
+        relay[pl.ds(dp, 1)] = msg[pl.ds(partner, 1)]
+
+    pl.semaphore_wait(barrier, jnp.where(near, xs * half - 1 + n_tp - 1, xs * half))
+
+    def send_row(row, peer, box, recv_sem):
         pltpu.make_async_remote_copy(
-            src_ref=msg.at[peer],
-            dst_ref=inbox.at[dp],
+            src_ref=msg.at[row],
+            dst_ref=box.at[dp],
             send_sem=dp_send,
-            recv_sem=dp_recv,
+            recv_sem=recv_sem,
             device_id={"dp": peer},
             device_id_type=MESH,
         ).start()
+
+    for peer, _ in near_peers:
+        send_row(peer, peer, inbox, dp_recv)
+
+    @pl.when(far)
+    def _():
+        peer, behind = own_column
+        pl.semaphore_signal(entered, inc=1, device_id={"dp": partner}, device_id_type=MESH)
+        send_row(peer, peer, inbox, dp_recv)
+        send_row(behind, peer, relay, relay_recv)
+
+    for peer, behind in near_peers:
+        send_row(behind, peer, relay, relay_recv)
 
     shifted = jnp.pad((ids_v[...] - tp * vocab).astype(F32), ((0, 6), (0, 0)))
     idt[...] = jnp.transpose(shifted).astype(jnp.int32)
@@ -145,21 +175,31 @@
     t1_src[6:8] = jnp.concatenate(parts, axis=0)
     t1[pl.ds(tp, 1)] = t1_src[...][None]
 
-    for peer in tp_peers:
-        pltpu.make_async_remote_copy(
-            src_ref=t1_src,
-            dst_ref=t1.at[tp],
-            send_sem=t1_send,
-            recv_sem=t1_recv,
-            device_id={"tensor": peer},
-            device_id_type=MESH,
-        ).start()
-
-    def all_but_one(ref, sem):
-        some = ref.at[pl.ds(0, ref.shape[0] - 1)]
+    def send_tensor(src, dst, send_sem, recv_sem):
+        for peer in tp_peers:
+            pltpu.make_async_remote_copy(
+                src_ref=src,
+                dst_ref=dst.at[tp],
+                send_sem=send_sem,
+                recv_sem=recv_sem,
+                device_id={"tensor": peer},
+                device_id_type=MESH,
+            ).start()
+
+    def first(ref, rows, sem):
+        some = ref.at[pl.ds(0, rows)]
         return pltpu.make_async_copy(some, some, sem)
 
-    all_but_one(inbox, dp_recv).wait()
+    @pl.when(near)
+    def _():
+        send_tensor(t1_src, t1, t1_send, t1_recv)
+        first(inbox, n_dp - 1, dp_recv).wait()
+
+    @pl.when(far)
+    def _():
+        first(inbox, n_dp, dp_recv).wait()
+        send_tensor(t1_src, t1, t1_send, t1_recv)
+
     got = inbox[...][:, 0, :]
     quiet[pl.ds(0, 64, stride=2), :] = got
     quiet[pl.ds(1, 64, stride=2), :] = pltpu.roll(got, 127, 1)
@@ -171,15 +211,13 @@
     t2_src[...] = pair(0)
     t2[pl.ds(tp, 1)] = t2_src[...][None]
 
-    for peer in tp_peers:
-        pltpu.make_async_remote_copy(
-            src_ref=t2_src,
-            dst_ref=t2.at[tp],
-            send_sem=t2_send,
-            recv_sem=t2_recv,
-            device_id={"tensor": peer},
-            device_id_type=MESH,
-        ).start()
+    send_tensor(t2_src, t2, t2_send, t2_recv)
+
+    @pl.when(near)
+    def _():
+        pl.semaphore_wait(entered, 1)
+        for peer in tp_peers:
+            pl.semaphore_signal(line_in, inc=1, device_id={"tensor": peer}, device_id_type=MESH)
 
     ref_rows, held_returns = pair(2), pair(4)
     same = (turned[12:13] == pid).astype(F32)
@@ -191,7 +229,7 @@
     var = (square - mean * summed) / floor
     whitened = (advantages - mean) * lax.rsqrt(var + 1.0)
 
-    all_but_one(t1, t1_recv).wait()
+    first(t1, n_tp - 1, t1_recv).wait()
     shards = t1[...]
     values = jnp.sum(shards[:, 6:8], axis=0)
     coeff = jnp.where(held_returns > 1e29, 0.0, 32.0 * (values - held_returns))
@@ -211,13 +249,36 @@
     policy = live * (surrogate + 0.1 * penalty)
     scale = 0.25 * live
 
-    all_but_one(t2, t2_recv).wait()
+    forward = pltpu.make_async_remote_copy(
+        src_ref=relay,
+        dst_ref=inbox,
+        send_sem=relay_send,
+        recv_sem=dp_recv,
+        device_id={"dp": partner},
+        device_id_type=MESH,
+    )
+
+    @pl.when(near)
+    def _():
+        pl.semaphore_wait(line_in, n_tp - 1)
+        first(relay, n_dp - 1, relay_recv).wait()
+        forward.start()
+
+    first(t2, n_tp - 1, t2_recv).wait()
     error = jnp.sum(t2[...], axis=0) - returns
     loss_out[...] = policy + scale * error * error
 
-    all_but_one(inbox, dp_send).wait()
-    all_but_one(t1, t1_send).wait()
-    all_but_one(t2, t2_send).wait()
+    first(t1, n_tp - 1, t1_send).wait()
+    first(t2, n_tp - 1, t2_send).wait()
+
+    @pl.when(near)
+    def _():
+        first(msg, n_dp - 2, dp_send).wait()
+        first(relay, n_dp, relay_send).wait()
+
+    @pl.when(far)
+    def _():
+        first(msg, n_dp, dp_send).wait()
 
 
 def finish(loss, grad, loss_out, grad_out, sems):
@@ -264,6 +325,7 @@
             vm((128, 128), F32),
             vm((64, 1, 128), F32),
             vm((64, 1, 128), F32),
+            vm((64, 1, 128), F32),
             vm((128, 128), F32),
             vm((128, 8), jnp.int32),
             vm((128, 128), F32),
@@ -272,6 +334,7 @@
             vm((seqs, length), F32),
             vm((2 * ys, seqs, length), F32),
             dma((4,)), dma((10,)), dma, dma, dma, dma, dma, dma,
+            dma, dma, pltpu.SemaphoreType.REGULAR, pltpu.SemaphoreType.REGULAR,
         ],
         compiler_params=pltpu.CompilerParams(collective_id=0, has_side_effects=True),
         name="ppo_all",

time: 40 us -> 34.3 us (0.86)
  Pallas kernels: 39.2 us -> 33.4 us
    pallas_call x1, Pallas kernels: 38.5 us -> 32.8 us  [per_device(): pl.pallas_call(functools.partial(kernel, xs, zs, ys, vocab), out_shape=(v...]
where the time goes in v3:
time: 34.3 us; the launch traced here: 34.1 us
  Pallas kernels  33.4 us (97%)
  between operations  0.64 us (2%)
    pallas_call x1, Pallas kernels, per_device(): pl.pallas_call(functools.partial(kernel, xs, zs, ys, vocab), out_shape=(v...  32.8 us
    pallas_call x1, Pallas kernels, per_device(): pl.pallas_call(finish, out_shape=(jax.ShapeDtypeStruct((seqs, length), F3...  0.69 us

profile of v3, /device:TPU:1, one launch (start us, length us, event | category | flops | bytes accessed | tf_op | source)
XLA Modules:
  0.0 34.1 jit_solution(14284121487474998156)
XLA Ops:
  0.6 32.8 %ppo_all.1 = (f32[2,128]{1,0:T(2,128)S(1)}, bf16[2,320,128]{2,1,0:T(8,128)(2,1)S(1)}) custom-call(bf16[2,128,4864]{2,1,0:T(8,128)(2,1)} %logits.1, s32[2,128]{1,0:T(2,128)} %ids.1, s32[2,128]{1,0:T(2,128)} %mask.1, s32[2]{0:T(128)} %lengths_in.1, s32[2]{0:T(128)} %prompt_in.1, f32[2,128]{1,0:T(2,128)} %old.1, bf16[2,128]{1,0:T(2,128)(2,1)} %bitcast.4, ...), custom_call_target="tpu_custom_call" | custom-call | tf_op jit(solution)/shard_map/ppo_all/pallas_call | solution.py:305
  33.4 0.7 %ppo_finish.1 = (f32[2,128]{1,0:T(2,128)}, bf16[2,320,128]{2,1,0:T(8,128)(2,1)}) custom-call(f32[2,128]{1,0:T(2,128)S(1)} %get-tuple-element.6.loss, bf16[2,320,128]{2,1,0:T(8,128)(2,1)S(1)} %get-tuple-element.7.grad), custom_call_target="tpu_custom_call" | custom-call | tf_op jit(solution)/shard_map/ppo_finish/pallas_call | solution.py:345

commit v4 on v3

--- a/solution.py
+++ b/solution.py
@@ -24,9 +24,9 @@
     logits, ids, mask, lengths_in, prompt_in, old, ref_t, adv, ret, critic, weight,
     loss_out, grad_out,
     lg, cr, ids_v, mask_v, old_v, ref_v, adv_v, ret_v, w_v, lengths, prompt_of,
-    stage, msg, inbox, relay, quiet, idt, stt, t1_src, t1, t2_src, t2,
+    stage, msg, inbox, relay, direct, quiet, idt, stt, t1_src, t1, t2_src, t2,
     lg_sem, in_sem, dp_send, dp_recv, t1_send, t1_recv, t2_send, t2_recv,
-    relay_send, relay_recv, entered, line_in,
+    relay_send, relay_recv, direct_send, direct_recv, entered, line_in,
 ):
     dp, tp = lax.axis_index("dp"), lax.axis_index("tensor")
     n_dp, n_tp = xs * zs, 2 * ys
@@ -36,7 +36,8 @@
         pltpu.make_async_copy(src, dst, in_sem.at[n])
         for n, (src, dst) in enumerate(
             [
-                (critic, cr), (weight, w_v), (ref_t, ref_v), (mask, mask_v), (adv, adv_v),
+                *((critic.at[j, r], cr.at[j, r]) for j in range(2) for r in (pl.ds(0, 160), pl.ds(160, 160))),
+                (weight, w_v), (ref_t, ref_v), (mask, mask_v), (adv, adv_v),
                 (lengths_in, lengths), (prompt_in, prompt_of), (ret, ret_v), (ids, ids_v), (old, old_v),
             ]
         )
@@ -55,8 +56,13 @@
     near_peers = [
         (at_x[x] + at_near[z], at_x[x] + (zs - 1 - at_near[z])) for x, z in far_first(xs, half)
     ]
-    own_column = (my_x * zs + at_near[0], my_x * zs + (zs - 1 - at_near[0]))
-
+    low, high = ys // 2 - 1, ys // 2 + 1
+    straight = jnp.logical_and(my_y >= low, my_y <= high)
+    in_low, in_high = 2 * low, 2 * high + 2
+    first_dp, first_tp = 0, 1
+    is_first = jnp.logical_and(dp == first_dp, tp == first_tp)
+    skips = jnp.logical_and(dp == first_dp, straight)
+    columns = [(z, x) for z in range(half) for x in sorted(range(xs), key=lambda d: -min(d, xs - d))]
     tp_peers = [at_y[y] + at_c[c] for y, c in far_first(ys, 2)]
 
     barrier = pltpu.get_barrier_semaphore()
@@ -68,6 +74,19 @@
         for peer in tp_peers:
             pl.semaphore_signal(barrier, inc=1, device_id={"tensor": peer}, device_id_type=MESH)
 
+    @pl.when(is_first)
+    def _():
+        for column in range(in_low, in_high):
+
+            def greet(i, carry):
+                place = {"dp": i, "tensor": column}
+                pl.semaphore_signal(barrier, inc=1, device_id=place, device_id_type=MESH)
+                return carry
+
+            lax.fori_loop(1, n_dp, greet, 0)
+
+    for copy in smalls:
+        copy.wait()
     chunks = []
     for b in range(2):
         for h in range(2):
@@ -76,8 +95,6 @@
                 pltpu.make_async_copy(logits.at[b, rows], lg.at[b, rows], lg_sem.at[b * 2 + h])
             )
             chunks[-1].start()
-    for copy in smalls:
-        copy.wait()
 
     row2 = lax.broadcasted_iota(jnp.int32, (2, 128), 0)
     lane2 = lax.broadcasted_iota(jnp.int32, (2, 128), 1)
@@ -113,12 +130,50 @@
     packed = stage[pl.ds(0, 64, stride=2), :] + pltpu.roll(stage[pl.ds(1, 64, stride=2), :], 16, 1)
     msg[...] = packed[:, None, :]
 
+    def read_logits():
+        shifted = jnp.pad((ids_v[...] - tp * vocab).astype(F32), ((0, 6), (0, 0)))
+        idt[...] = jnp.transpose(shifted).astype(jnp.int32)
+        stt[...] = jnp.zeros((128, 128), F32)
+        lane = lax.broadcasted_iota(jnp.int32, (BLOCK, 128), 1)
+        for b in range(2):
+            for h in range(2):
+                chunks[b * 2 + h].wait()
+
+                def token_block(i, carry):
+                    rows = pl.ds(pl.multiple_of(h * 64 + i * BLOCK, BLOCK), BLOCK)
+                    top = lg[b, rows, pl.ds(0, 128)]
+                    for c in range(1, vocab // 128):
+                        top = jnp.maximum(top, lg[b, rows, pl.ds(c * 128, 128)])
+                    top = jnp.max(top.astype(F32), axis=1, keepdims=True)
+                    tops = jnp.broadcast_to(top, (BLOCK, 128))
+                    wanted = jnp.broadcast_to(idt[rows, b : b + 1], (BLOCK, 128))
+                    total = jnp.zeros((BLOCK, 128), F32)
+                    found = jnp.zeros((BLOCK, 128), F32)
+                    for c in range(vocab // 128):
+                        x = lg[b, rows, pl.ds(c * 128, 128)].astype(F32)
+                        total = total + jnp.exp(x - tops)
+                        found = jnp.where(wanted == lane + c * 128, x, found)
+                    stt[rows, b : b + 1] = top
+                    stt[rows, 2 + b : 3 + b] = jnp.sum(total, axis=1, keepdims=True)
+                    stt[rows, 4 + b : 5 + b] = jnp.sum(found, axis=1, keepdims=True)
+                    return carry
+
+                lax.fori_loop(0, 64 // BLOCK, token_block, 0)
+        t1_src[0:6] = jnp.transpose(stt[...])[0:6]
+        t1_src[6:8] = jnp.concatenate(parts, axis=0)
+        t1[pl.ds(tp, 1)] = t1_src[...][None]
+
     @pl.when(near)
     def _():
         inbox[pl.ds(dp, 1)] = msg[pl.ds(dp, 1)]
         relay[pl.ds(dp, 1)] = msg[pl.ds(partner, 1)]
 
-    pl.semaphore_wait(barrier, jnp.where(near, xs * half - 1 + n_tp - 1, xs * half))
+    @pl.when(my_z < half // 2)
+    def _():
+        read_logits()
+
+    guests = jnp.where(near, xs * half - 1 + n_tp - 1, xs * half)
+    pl.semaphore_wait(barrier, guests + jnp.where(straight, 1, 0) - jnp.where(skips, 1, 0))
 
     def send_row(row, peer, box, recv_sem):
         pltpu.make_async_remote_copy(
@@ -130,61 +185,49 @@
             device_id_type=MESH,
         ).start()
 
-    for peer, _ in near_peers:
-        send_row(peer, peer, inbox, dp_recv)
+    @pl.when(straight)
+    def _():
+        pltpu.make_async_remote_copy(
+            src_ref=msg.at[first_dp],
+            dst_ref=direct.at[tp - in_low, dp],
+            send_sem=direct_send,
+            recv_sem=direct_recv,
+            device_id={"dp": first_dp, "tensor": first_tp},
+            device_id_type=MESH,
+        ).start()
 
     @pl.when(far)
     def _():
-        peer, behind = own_column
         pl.semaphore_signal(entered, inc=1, device_id={"dp": partner}, device_id_type=MESH)
-        send_row(peer, peer, inbox, dp_recv)
-        send_row(behind, peer, relay, relay_recv)
-
-    for peer, behind in near_peers:
-        send_row(behind, peer, relay, relay_recv)
-
-    shifted = jnp.pad((ids_v[...] - tp * vocab).astype(F32), ((0, 6), (0, 0)))
-    idt[...] = jnp.transpose(shifted).astype(jnp.int32)
-    stt[...] = jnp.zeros((128, 128), F32)
-    lane = lax.broadcasted_iota(jnp.int32, (BLOCK, 128), 1)
-    for b in range(2):
-        for h in range(2):
-            chunks[b * 2 + h].wait()
-
-            def token_block(i, carry):
-                rows = pl.ds(pl.multiple_of(h * 64 + i * BLOCK, BLOCK), BLOCK)
-                top = lg[b, rows, pl.ds(0, 128)]
-                for c in range(1, vocab // 128):
-                    top = jnp.maximum(top, lg[b, rows, pl.ds(c * 128, 128)])
-                top = jnp.max(top.astype(F32), axis=1, keepdims=True)
-                tops = jnp.broadcast_to(top, (BLOCK, 128))
-                wanted = jnp.broadcast_to(idt[rows, b : b + 1], (BLOCK, 128))
-                total = jnp.zeros((BLOCK, 128), F32)
-                found = jnp.zeros((BLOCK, 128), F32)
-                for c in range(vocab // 128):
-                    x = lg[b, rows, pl.ds(c * 128, 128)].astype(F32)
-                    total = total + jnp.exp(x - tops)
-                    found = jnp.where(wanted == lane + c * 128, x, found)
-                stt[rows, b : b + 1] = top
-                stt[rows, 2 + b : 3 + b] = jnp.sum(total, axis=1, keepdims=True)
-                stt[rows, 4 + b : 5 + b] = jnp.sum(found, axis=1, keepdims=True)
-                return carry
-
-            lax.fori_loop(0, 64 // BLOCK, token_block, 0)
-    t1_src[0:6] = jnp.transpose(stt[...])[0:6]
-    t1_src[6:8] = jnp.concatenate(parts, axis=0)
-    t1[pl.ds(tp, 1)] = t1_src[...][None]
-
-    def send_tensor(src, dst, send_sem, recv_sem):
+        for z, x in columns:
+            send_row(at_x[x] + z, at_x[x] + z, inbox, dp_recv)
+        for z, x in columns:
+            send_row(at_x[x] + zs - 1 - z, at_x[x] + z, relay, relay_recv)
+
+    @pl.when(near)
+    def _():
+        for peer, _ in near_peers:
+            send_row(peer, peer, inbox, dp_recv)
+        for peer, behind in near_peers:
+            send_row(behind, peer, relay, relay_recv)
+
+    @pl.when(my_z >= half // 2)
+    def _():
+        read_logits()
+
+    def send_one(src, dst, send_sem, recv_sem, peer):
+        pltpu.make_async_remote_copy(
+            src_ref=src,
+            dst_ref=dst.at[tp],
+            send_sem=send_sem,
+            recv_sem=recv_sem,
+            device_id={"tensor": peer},
+            device_id_type=MESH,
+        ).start()
+
+    def send_t1():
         for peer in tp_peers:
-            pltpu.make_async_remote_copy(
-                src_ref=src,
-                dst_ref=dst.at[tp],
-                send_sem=send_sem,
-                recv_sem=recv_sem,
-                device_id={"tensor": peer},
-                device_id_type=MESH,
-            ).start()
+            send_one(t1_src, t1, t1_send, t1_recv, peer)
 
     def first(ref, rows, sem):
         some = ref.at[pl.ds(0, rows)]
@@ -192,34 +235,52 @@
 
     @pl.when(near)
     def _():
-        send_tensor(t1_src, t1, t1_send, t1_recv)
-        first(inbox, n_dp - 1, dp_recv).wait()
-
-    @pl.when(far)
-    def _():
-        first(inbox, n_dp, dp_recv).wait()
-        send_tensor(t1_src, t1, t1_send, t1_recv)
-
-    got = inbox[...][:, 0, :]
-    quiet[pl.ds(0, 64, stride=2), :] = got
-    quiet[pl.ds(1, 64, stride=2), :] = pltpu.roll(got, 127, 1)
-    turned = jnp.transpose(quiet[...])
-
-    def pair(k):
-        return jnp.concatenate([turned[k : k + 1], turned[16 + k : 17 + k]], axis=0)
-
-    t2_src[...] = pair(0)
-    t2[pl.ds(tp, 1)] = t2_src[...][None]
-
-    send_tensor(t2_src, t2, t2_send, t2_recv)
-
-    @pl.when(near)
-    def _():
+        send_t1()
         pl.semaphore_wait(entered, 1)
         for peer in tp_peers:
             pl.semaphore_signal(line_in, inc=1, device_id={"tensor": peer}, device_id_type=MESH)
-
-    ref_rows, held_returns = pair(2), pair(4)
+        first(inbox, n_dp - 1, dp_recv).wait()
+
+    @pl.when(far)
+    def _():
+        first(inbox, n_dp, dp_recv).wait()
+        send_t1()
+
+    def turn(got):
+        quiet[pl.ds(0, 64, stride=2), :] = got
+        quiet[pl.ds(1, 64, stride=2), :] = pltpu.roll(got, 127, 1)
+        return jnp.transpose(quiet[...])
+
+    def pair(turned, k):
+        return jnp.concatenate([turned[k : k + 1], turned[16 + k : 17 + k]], axis=0)
+
+    turned = turn(inbox[...][:, 0, :])
+    t2_src[...] = pair(turned, 0)
+    t2[pl.ds(tp, 1)] = t2_src[...][None]
+
+    for peer in tp_peers:
+
+        @pl.when(jnp.logical_not(jnp.logical_and(skips, peer == first_tp)))
+        def _():
+            send_one(t2_src, t2, t2_send, t2_recv, peer)
+
+
+    forward = pltpu.make_async_remote_copy(
+        src_ref=relay,
+        dst_ref=inbox,
+        send_sem=relay_send,
+        recv_sem=dp_recv,
+        device_id={"dp": partner},
+        device_id_type=MESH,
+    )
+
+    @pl.when(near)
+    def _():
+        pl.semaphore_wait(line_in, n_tp - 1)
+        first(relay, n_dp - 1, relay_recv).wait()
+        forward.start()
+
+    ref_rows, held_returns = pair(turned, 2), pair(turned, 4)
     same = (turned[12:13] == pid).astype(F32)
     count = jnp.sum(same * turned[6:7], axis=1, keepdims=True)
     summed = jnp.sum(same * turned[8:9], axis=1, keepdims=True)
@@ -249,27 +310,34 @@
     policy = live * (surrogate + 0.1 * penalty)
     scale = 0.25 * live
 
-    forward = pltpu.make_async_remote_copy(
-        src_ref=relay,
-        dst_ref=inbox,
-        send_sem=relay_send,
-        recv_sem=dp_recv,
-        device_id={"dp": partner},
-        device_id_type=MESH,
-    )
-
-    @pl.when(near)
-    def _():
-        pl.semaphore_wait(line_in, n_tp - 1)
-        first(relay, n_dp - 1, relay_recv).wait()
-        forward.start()
-
-    first(t2, n_tp - 1, t2_recv).wait()
+    @pl.when(is_first)
+    def _():
+        first(t2, n_tp - 1 - (in_high - in_low), t2_recv).wait()
+        pltpu.make_async_copy(direct, direct, direct_recv).wait()
+        t2[in_low] = pair(turn(jnp.sum(direct[...], axis=0)[:, 0, :]), 0)
+        for column in range(in_low + 1, in_high):
+            t2[column] = jnp.zeros((2, 128), F32)
+
+    @pl.when(jnp.logical_not(is_first))
+    def _():
+        first(t2, n_tp - 1, t2_recv).wait()
+
     error = jnp.sum(t2[...], axis=0) - returns
     loss_out[...] = policy + scale * error * error
 
     first(t1, n_tp - 1, t1_send).wait()
-    first(t2, n_tp - 1, t2_send).wait()
+
+    @pl.when(skips)
+    def _():
+        first(t2, n_tp - 2, t2_send).wait()
+
+    @pl.when(jnp.logical_not(skips))
+    def _():
+        first(t2, n_tp - 1, t2_send).wait()
+
+    @pl.when(straight)
+    def _():
+        first(msg, 1, direct_send).wait()
 
     @pl.when(near)
     def _():
@@ -326,6 +394,7 @@
             vm((64, 1, 128), F32),
             vm((64, 1, 128), F32),
             vm((64, 1, 128), F32),
+            vm((6, 64, 1, 128), F32),
             vm((128, 128), F32),
             vm((128, 8), jnp.int32),
             vm((128, 128), F32),
@@ -333,8 +402,8 @@
             vm((2 * ys, 8, 128), F32),
             vm((seqs, length), F32),
             vm((2 * ys, seqs, length), F32),
-            dma((4,)), dma((10,)), dma, dma, dma, dma, dma, dma,
-            dma, dma, pltpu.SemaphoreType.REGULAR, pltpu.SemaphoreType.REGULAR,
+            dma((4,)), dma((13,)), dma, dma, dma, dma, dma, dma,
+            dma, dma, dma, dma, pltpu.SemaphoreType.REGULAR, pltpu.SemaphoreType.REGULAR,
         ],
         compiler_params=pltpu.CompilerParams(collective_id=0, has_side_effects=True),
         name="ppo_all",

time: 34.3 us -> 32.9 us (0.959)
  Pallas kernels: 33.4 us -> 32.1 us
    pallas_call x1, Pallas kernels: 32.8 us -> 31.4 us  [per_device(): pl.pallas_call(functools.partial(kernel, xs, zs, ys, vocab), out_shape=(v...]
where the time goes in v4:
time: 32.9 us; the launch traced here: 32.7 us
  Pallas kernels  32.1 us (98%)
  between operations  0.64 us (2%)
    pallas_call x1, Pallas kernels, per_device(): pl.pallas_call(functools.partial(kernel, xs, zs, ys, vocab), out_shape=(v...  31.4 us
    pallas_call x1, Pallas kernels, per_device(): pl.pallas_call(finish, out_shape=(jax.ShapeDtypeStruct((seqs, length), F3...  0.69 us

profile of v4, /device:TPU:1, one launch (start us, length us, event | category | flops | bytes accessed | tf_op | source)
XLA Modules:
  0.0 32.7 jit_solution(10445089808868365600)
XLA Ops:
  0.6 31.4 %ppo_all.1 = (f32[2,128]{1,0:T(2,128)S(1)}, bf16[2,320,128]{2,1,0:T(8,128)(2,1)S(1)}) custom-call(bf16[2,128,4864]{2,1,0:T(8,128)(2,1)} %logits.1, s32[2,128]{1,0:T(2,128)} %ids.1, s32[2,128]{1,0:T(2,128)} %mask.1, s32[2]{0:T(128)} %lengths_in.1, s32[2]{0:T(128)} %prompt_in.1, f32[2,128]{1,0:T(2,128)} %old.1, bf16[2,128]{1,0:T(2,128)(2,1)} %bitcast.4, ...), custom_call_target="tpu_custom_call" | custom-call | tf_op jit(solution)/shard_map/ppo_all/pallas_call | solution.py:373
  32.0 0.7 %ppo_finish.1 = (f32[2,128]{1,0:T(2,128)}, bf16[2,320,128]{2,1,0:T(8,128)(2,1)}) custom-call(f32[2,128]{1,0:T(2,128)S(1)} %get-tuple-element.6.loss, bf16[2,320,128]{2,1,0:T(8,128)(2,1)S(1)} %get-tuple-element.7.grad), custom_call_target="tpu_custom_call" | custom-call | tf_op jit(solution)/shard_map/ppo_finish/pallas_call | solution.py:414

commit v5 on v4

--- a/solution.py
+++ b/solution.py
@@ -24,9 +24,9 @@
     logits, ids, mask, lengths_in, prompt_in, old, ref_t, adv, ret, critic, weight,
     loss_out, grad_out,
     lg, cr, ids_v, mask_v, old_v, ref_v, adv_v, ret_v, w_v, lengths, prompt_of,
-    stage, msg, inbox, relay, direct, quiet, idt, stt, t1_src, t1, t2_src, t2,
+    stage, msg, inbox, relay, block, direct, quiet, idt, stt, t1_src, t1, t2_src, t2,
     lg_sem, in_sem, dp_send, dp_recv, t1_send, t1_recv, t2_send, t2_recv,
-    relay_send, relay_recv, direct_send, direct_recv, entered, line_in,
+    relay_send, block_recv, direct_send, direct_recv, entered, line_in,
 ):
     dp, tp = lax.axis_index("dp"), lax.axis_index("tensor")
     n_dp, n_tp = xs * zs, 2 * ys
@@ -53,13 +53,13 @@
     near, far = my_z < half, my_z >= half
     partner = my_x * zs + (zs - 1 - my_z)
     at_near = [lax.rem(my_z + d, half) for d in range(half)]
-    near_peers = [
-        (at_x[x] + at_near[z], at_x[x] + (zs - 1 - at_near[z])) for x, z in far_first(xs, half)
-    ]
-    low, high = ys // 2 - 1, ys // 2 + 1
-    straight = jnp.logical_and(my_y >= low, my_y <= high)
+    near_peers = [(at_x[x] + at_near[z], at_x[x] // 2 + at_near[z]) for x, z in far_first(xs, half)]
+    low, high = ys // 2 - 1, ys // 2 + 2
+    first_dp, first_tp = 0, 1
     in_low, in_high = 2 * low, 2 * high + 2
-    first_dp, first_tp = 0, 1
+    afar = jnp.logical_and(my_y >= low, my_y <= high)
+    straight = jnp.logical_or(afar, tp == 0)
+    sources = [0, *range(in_low, in_high)]
     is_first = jnp.logical_and(dp == first_dp, tp == first_tp)
     skips = jnp.logical_and(dp == first_dp, straight)
     columns = [(z, x) for z in range(half) for x in sorted(range(xs), key=lambda d: -min(d, xs - d))]
@@ -76,7 +76,7 @@
 
     @pl.when(is_first)
     def _():
-        for column in range(in_low, in_high):
+        for column in sources:
 
             def greet(i, carry):
                 place = {"dp": i, "tensor": column}
@@ -107,10 +107,10 @@
         return jnp.broadcast_to(jnp.sum(column, axis=1, keepdims=True), (2, 128))
 
     feats = w_v.shape[0]
-    w_row = jnp.pad(w_v[...].astype(F32).reshape(1, feats), ((0, 0), (0, -feats % 128)))
-    w_all = jnp.transpose(jnp.broadcast_to(w_row, (128, w_row.shape[1])))[:feats]
+    w_row = w_v[...].reshape(1, feats)
     parts = [
-        jnp.sum(cr[j].astype(F32) * w_all, axis=0, keepdims=True) for j in range(2)
+        jnp.dot(jnp.broadcast_to(w_row, (16, feats)), cr[j], preferred_element_type=F32)[:1]
+        for j in range(2)
     ]
     pid = jnp.where(row2 == 0, prompt_of[0], prompt_of[1]).astype(F32)
     lines = jnp.concatenate(
@@ -128,7 +128,10 @@
     )
     stage[...] = jnp.transpose(lines)
     packed = stage[pl.ds(0, 64, stride=2), :] + pltpu.roll(stage[pl.ds(1, 64, stride=2), :], 16, 1)
-    msg[...] = packed[:, None, :]
+    for x in range(xs):
+        for z in range(half):
+            for side, row in enumerate((x * zs + z, x * zs + zs - 1 - z)):
+                msg[x * half + z, side : side + 1] = packed[row : row + 1]
 
     def read_logits():
         shifted = jnp.pad((ids_v[...] - tp * vocab).astype(F32), ((0, 6), (0, 0)))
@@ -165,8 +168,7 @@
 
     @pl.when(near)
     def _():
-        inbox[pl.ds(dp, 1)] = msg[pl.ds(dp, 1)]
-        relay[pl.ds(dp, 1)] = msg[pl.ds(partner, 1)]
+        inbox[pl.ds(dp, 1)] = msg[pl.ds(my_x * half + my_z, 1)]
 
     @pl.when(my_z < half // 2)
     def _():
@@ -175,12 +177,12 @@
     guests = jnp.where(near, xs * half - 1 + n_tp - 1, xs * half)
     pl.semaphore_wait(barrier, guests + jnp.where(straight, 1, 0) - jnp.where(skips, 1, 0))
 
-    def send_row(row, peer, box, recv_sem):
+    def send_rows(place, peer):
         pltpu.make_async_remote_copy(
-            src_ref=msg.at[row],
-            dst_ref=box.at[dp],
+            src_ref=msg.at[place],
+            dst_ref=inbox.at[dp],
             send_sem=dp_send,
-            recv_sem=recv_sem,
+            recv_sem=dp_recv,
             device_id={"dp": peer},
             device_id_type=MESH,
         ).start()
@@ -189,7 +191,7 @@
     def _():
         pltpu.make_async_remote_copy(
             src_ref=msg.at[first_dp],
-            dst_ref=direct.at[tp - in_low, dp],
+            dst_ref=direct.at[jnp.where(afar, tp - in_low + 1, 0), dp],
             send_sem=direct_send,
             recv_sem=direct_recv,
             device_id={"dp": first_dp, "tensor": first_tp},
@@ -200,20 +202,20 @@
     def _():
         pl.semaphore_signal(entered, inc=1, device_id={"dp": partner}, device_id_type=MESH)
         for z, x in columns:
-            send_row(at_x[x] + z, at_x[x] + z, inbox, dp_recv)
-        for z, x in columns:
-            send_row(at_x[x] + zs - 1 - z, at_x[x] + z, relay, relay_recv)
-
-    @pl.when(near)
-    def _():
-        for peer, _ in near_peers:
-            send_row(peer, peer, inbox, dp_recv)
-        for peer, behind in near_peers:
-            send_row(behind, peer, relay, relay_recv)
+            send_rows(at_x[x] // 2 + z, at_x[x] + z)
+
+    @pl.when(near)
+    def _():
+        for peer, place in near_peers:
+            send_rows(place, peer)
 
     @pl.when(my_z >= half // 2)
     def _():
         read_logits()
+
+    def take(got):
+        quiet[pl.ds(0, 64, stride=2), :] = got
+        quiet[pl.ds(1, 64, stride=2), :] = pltpu.roll(got, 127, 1)
 
     def send_one(src, dst, send_sem, recv_sem, peer):
         pltpu.make_async_remote_copy(
@@ -240,36 +242,40 @@
         for peer in tp_peers:
             pl.semaphore_signal(line_in, inc=1, device_id={"tensor": peer}, device_id_type=MESH)
         first(inbox, n_dp - 1, dp_recv).wait()
+        take(inbox[...][:, 0, :])
 
     @pl.when(far)
     def _():
-        first(inbox, n_dp, dp_recv).wait()
+        first(block, n_dp, block_recv).wait()
+        take(block[...][:, 0, :])
         send_t1()
-
-    def turn(got):
-        quiet[pl.ds(0, 64, stride=2), :] = got
-        quiet[pl.ds(1, 64, stride=2), :] = pltpu.roll(got, 127, 1)
-        return jnp.transpose(quiet[...])
 
     def pair(turned, k):
         return jnp.concatenate([turned[k : k + 1], turned[16 + k : 17 + k]], axis=0)
 
-    turned = turn(inbox[...][:, 0, :])
+    turned = jnp.transpose(quiet[...])
     t2_src[...] = pair(turned, 0)
     t2[pl.ds(tp, 1)] = t2_src[...][None]
 
-    for peer in tp_peers:
-
-        @pl.when(jnp.logical_not(jnp.logical_and(skips, peer == first_tp)))
-        def _():
+    @pl.when(skips)
+    def _():
+        for peer in tp_peers:
+
+            @pl.when(peer != first_tp)
+            def _():
+                send_one(t2_src, t2, t2_send, t2_recv, peer)
+
+    @pl.when(jnp.logical_not(skips))
+    def _():
+        for peer in tp_peers:
             send_one(t2_src, t2, t2_send, t2_recv, peer)
 
 
     forward = pltpu.make_async_remote_copy(
         src_ref=relay,
-        dst_ref=inbox,
+        dst_ref=block,
         send_sem=relay_send,
-        recv_sem=dp_recv,
+        recv_sem=block_recv,
         device_id={"dp": partner},
         device_id_type=MESH,
     )
@@ -277,7 +283,7 @@
     @pl.when(near)
     def _():
         pl.semaphore_wait(line_in, n_tp - 1)
-        first(relay, n_dp - 1, relay_recv).wait()
+        relay[...] = inbox[...][:, 1:2, :]
         forward.start()
 
     ref_rows, held_returns = pair(turned, 2), pair(turned, 4)
@@ -293,6 +299,8 @@
     first(t1, n_tp - 1, t1_recv).wait()
     shards = t1[...]
     values = jnp.sum(shards[:, 6:8], axis=0)
+    w_wide = jnp.pad(w_row.astype(F32), ((0, 0), (0, -feats % 128)))
+    w_all = jnp.transpose(jnp.broadcast_to(w_wide, (128, w_wide.shape[1])))[:feats]
     coeff = jnp.where(held_returns > 1e29, 0.0, 32.0 * (values - held_returns))
     for j in range(2):
         grad_out[j] = (w_all * coeff[j : j + 1]).astype(jnp.bfloat16)
@@ -312,10 +320,11 @@
 
     @pl.when(is_first)
     def _():
-        first(t2, n_tp - 1 - (in_high - in_low), t2_recv).wait()
+        first(t2, n_tp - 1 - len(sources), t2_recv).wait()
         pltpu.make_async_copy(direct, direct, direct_recv).wait()
-        t2[in_low] = pair(turn(jnp.sum(direct[...], axis=0)[:, 0, :]), 0)
-        for column in range(in_low + 1, in_high):
+        take(jnp.sum(direct[...], axis=0)[:, 0, :])
+        t2[0] = pair(jnp.transpose(quiet[...]), 0)
+        for column in sources[1:]:
             t2[column] = jnp.zeros((2, 128), F32)
 
     @pl.when(jnp.logical_not(is_first))
@@ -341,12 +350,12 @@
 
     @pl.when(near)
     def _():
-        first(msg, n_dp - 2, dp_send).wait()
+        first(msg, n_dp // 2 - 1, dp_send).wait()
         first(relay, n_dp, relay_send).wait()
 
     @pl.when(far)
     def _():
-        first(msg, n_dp, dp_send).wait()
+        first(msg, n_dp // 2, dp_send).wait()
 
 
 def finish(loss, grad, loss_out, grad_out, sems):
@@ -391,10 +400,11 @@
             pltpu.SMEM((seqs,), jnp.int32),
             pltpu.SMEM((seqs,), jnp.int32),
             vm((128, 128), F32),
+            vm((32, 2, 128), F32),
+            vm((64, 2, 128), F32),
             vm((64, 1, 128), F32),
             vm((64, 1, 128), F32),
-            vm((64, 1, 128), F32),
-            vm((6, 64, 1, 128), F32),
+            vm((9, 64, 2, 128), F32),
             vm((128, 128), F32),
             vm((128, 8), jnp.int32),
             vm((128, 128), F32),

time: 32.9 us -> 32.8 us (level); the launches traced: 32.7 us -> 32.2 us
  Pallas kernels: 32.1 us -> 31.6 us
    pallas_call x1, Pallas kernels: 31.4 us -> 30.9 us  [per_device(): pl.pallas_call(functools.partial(kernel, xs, zs, ys, vocab), out_shape=(v...]
where the time goes in v5:
time: 32.8 us; the launch traced here: 32.2 us
  Pallas kernels  31.6 us (96%)
  between operations  0.64 us (2%)
    pallas_call x1, Pallas kernels, per_device(): pl.pallas_call(functools.partial(kernel, xs, zs, ys, vocab), out_shape=(v...  30.9 us
    pallas_call x1, Pallas kernels, per_device(): pl.pallas_call(finish, out_shape=(jax.ShapeDtypeStruct((seqs, length), F3...  0.69 us

profile of v5, /device:TPU:1, one launch (start us, length us, event | category | flops | bytes accessed | tf_op | source)
XLA Modules:
  0.0 32.2 jit_solution(6465777493428429969)
XLA Ops:
  0.6 30.9 %ppo_all.1 = (f32[2,128]{1,0:T(2,128)S(1)}, bf16[2,320,128]{2,1,0:T(8,128)(2,1)S(1)}) custom-call(bf16[2,128,4864]{2,1,0:T(8,128)(2,1)} %logits.1, s32[2,128]{1,0:T(2,128)} %ids.1, s32[2,128]{1,0:T(2,128)} %mask.1, s32[2]{0:T(128)} %lengths_in.1, s32[2]{0:T(128)} %prompt_in.1, f32[2,128]{1,0:T(2,128)} %old.1, bf16[2,128]{1,0:T(2,128)(2,1)} %bitcast.4, ...), custom_call_target="tpu_custom_call" | custom-call | tf_op jit(solution)/shard_map/ppo_all/pallas_call | solution.py:382
  31.6 0.7 %ppo_finish.1 = (f32[2,128]{1,0:T(2,128)}, bf16[2,320,128]{2,1,0:T(8,128)(2,1)}) custom-call(f32[2,128]{1,0:T(2,128)S(1)} %get-tuple-element.6.loss, bf16[2,320,128]{2,1,0:T(8,128)(2,1)S(1)} %get-tuple-element.7.grad), custom_call_target="tpu_custom_call" | custom-call | tf_op jit(solution)/shard_map/ppo_finish/pallas_call | solution.py:424
